TPU v7x, 32 devices: a whole 2x2x4 slice. The times are simulated.
32 devices in a mesh: rows: 8 (over y, x, core), feat: 4 (over z).
Axes of the slice: x: 2, y: 2, z: 4, core: 2. Of those that a mesh axis runs over, the one named last changes fastest.
Arguments:
- bins: int32 [16384, 1024], P('rows', 'feat'), may hold values from 0 to 255
- node_ids: int32 [2, 16384], P(None, 'rows'), may hold values from 0 to 15
- boot_counts: int32 [2, 16384], P(None, 'rows'), may hold values from 0 to 3
- gradient: bfloat16 [16384], P('rows'), may hold values from -6 to 6
Outputs:
- gains: float32 [4, 256, 2, 16, 256], P('feat', 'rows')
- best_gain: float32 [2, 16], replicated
All inputs are finite; a program needn't handle non-finite values.
Results may differ from a plain program's by a relative error of at most 0.003.
Values may be sent and summed in bfloat16 or wider, within the bound.
A program may use at most 64 MiB of HBM per device.

v0:
```python
import jax
import jax.numpy as jnp
from jax import lax
from jax.sharding import PartitionSpec as P

BINS = 256
NODES = 16


ridge = 1.0


def split_gains(hist):
    left_grad = jnp.cumsum(hist[:, :, 0], axis=-1)
    left_count = jnp.cumsum(hist[:, :, 1], axis=-1)
    total_grad = left_grad[..., -1:]
    total_count = left_count[..., -1:]
    right_grad = total_grad - left_grad
    right_count = total_count - left_count
    return (
        left_grad * left_grad / (left_count + ridge)
        + right_grad * right_grad / (right_count + ridge)
        - total_grad * total_grad / (total_count + ridge)
    )


def build_columns(node_ids, boot_counts, gradient):
    row_count = node_ids.shape[1]
    tree_count = node_ids.shape[0]
    weighted = (boot_counts.astype(jnp.float32) * gradient.astype(jnp.float32)[None, :]).astype(
        jnp.bfloat16
    )
    node_hot = (node_ids[:, :, None] == jnp.arange(NODES, dtype=jnp.int32)[None, None, :]).astype(
        jnp.bfloat16
    )
    counts_low = boot_counts.astype(jnp.bfloat16)
    columns = jnp.stack(
        [weighted[:, :, None] * node_hot, counts_low[:, :, None] * node_hot], axis=1
    )
    columns = jnp.transpose(columns, (2, 0, 1, 3))
    return columns.reshape(row_count, tree_count * 2 * NODES)


def per_device(bins, node_ids, boot_counts, gradient):
    row_count, feat_local = bins.shape
    tree_count = node_ids.shape[0]
    shards = lax.axis_size("rows")
    owned = feat_local // shards
    owned_bins = lax.all_to_all(bins, "rows", split_axis=1, concat_axis=0, tiled=True)
    labels = lax.all_gather(
        jnp.concatenate([node_ids, boot_counts], axis=0), "rows", axis=1, tiled=True
    )
    all_gradient = lax.all_gather(gradient, "rows", axis=0, tiled=True)
    flat = build_columns(labels[:tree_count], labels[tree_count:], all_gradient)
    total_rows = owned_bins.shape[0]
    factor = max(
        [g for g in range(1, shards + 1) if shards % g == 0 and (g == 1 or g * row_count <= 4096)]
    )
    block_rows = row_count * factor
    turns = total_rows // block_rows
    width = flat.shape[1]

    def add_block(turn, total):
        first = turn * block_rows
        picked = lax.dynamic_slice_in_dim(owned_bins, first, block_rows, 0)
        cols = lax.dynamic_slice_in_dim(flat, first, block_rows, 0)
        bin_hot = (picked[:, :, None] == jnp.arange(BINS, dtype=jnp.int32)[None, None, :]).astype(
            jnp.bfloat16
        )
        return total + jnp.einsum("rk,rjb->jkb", cols, bin_hot, preferred_element_type=jnp.float32)

    local = lax.fori_loop(0, turns, add_block, jnp.zeros((owned, width, BINS), jnp.float32))
    hist = local.reshape(owned, tree_count, 2, NODES, BINS)
    gain = split_gains(hist)
    local_best = jnp.max(gain, axis=(0, 3))
    best_gain = lax.pmax(local_best, ("rows", "feat"))
    return (gain[None], best_gain)


def solution(mesh):
    in_specs = (P("rows", "feat"), P(None, "rows"), P(None, "rows"), P("rows"))
    out_specs = (P("feat", "rows", None, None, None), P())
    return jax.shard_map(
        per_device, mesh=mesh, in_specs=in_specs, out_specs=out_specs, check_vma=False
    )
```

profile of v0, /device:TPU:0, one launch (start us, length us, event | category | flops | bytes accessed | tf_op | source)
XLA Modules:
  0.0 312.3 jit_solution(10422046821901788328)
XLA Ops:
  0.6 3.0 copy.66
  3.6 5.3 %all-to-all-start = ((s32[2048,8,32]{0,2,1:T(8,128)}), s32[2048,8,32]{0,2,1:T(8,128)}, u32[]{:S(2)}, u32[]{:S(2)}) async-start(s32[2048,8,32]{0,2,1:T(8,128)} %bitcast), calls=%async_computation | async-start | bytes 4194304 | tf_op jit(solution)/shard_map/all_to_all | solution.py:49
  9.0 30.2 %all_gather.6 = s32[4,16384]{1,0:T(4,128)S(1)} all-gather(s32[4,2048]{1,0:T(4,128)S(1)} %pad_add_fusion), channel_id=1, replica_groups=mesh['rows'=8,'feat'=4] {'rows'}, dimensions={1}, use_global_device_ids=true | all-gather | bytes 294912 | tf_op jit(solution)/shard_map/all_gather | solution.py:50
  39.2 0.1 slice_convert_fusion
  39.3 8.2 %all_gather.7 = bf16[16384]{0:T(1024)(128)(2,1)S(1)} all-gather(bf16[2048]{0:T(1024)(128)(2,1)S(1)} %copy-done.4), channel_id=1, replica_groups=mesh['rows'=8,'feat'=4] {'rows'}, dimensions={0}, use_global_device_ids=true | all-gather | bytes 36864 | tf_op jit(solution)/shard_map/all_gather | solution.py:53
  47.5 0.1 multiply_convert_fusion
  47.6 0.3 fusion.6
  48.0 0.2 pad_maximum_fusion
  48.2 3.2 %copy.94 = s32[8,4,8,2048]{3,2,0,1:T(8,128)} copy(s32[8,4,8,2048]{3,2,1,0:T(8,128)} %bitcast.17) | data formatting | bytes 4194304 | tf_op jit(solution)/shard_map/all_to_all | solution.py:49
  51.4 125.3 %while.14 = (s32[]{:T(128)}, f32[32,64,256]{2,1,0:T(8,128)}, s32[16384,32]{0,1:T(8,128)}, bf16[16384,64]{0,1:T(8,128)(2,1)S(1)}, s32[]{:T(128)}, /*index=5*/s32[]{:T(128)}, s32[]{:T(128)}, s32[]{:T(128)}) while((s32[]{:T(128)}, f32[32,64,256]{2,1,0:T(8,128)}, s32[16384,32]{0,1:T(8,128)}, bf16[16384,64]{0,1:T(8,128)(2,1)S(1)}, ...), condition=%wide.region_1.0_spmd.clone, body=%wide.region_0.0_spmd.clone.sunk | while | flops 4329570304 | bytes 7340181 | solution.py:72
  51.4 1.1 constant_dynamic-slice_fusion.2
  52.5 29.7 %bitcast_add_fusion.2 = f32[32,64,256]{2,1,0:T(8,128)} fusion(f32[32,64,256]{2,1,0:T(8,128)} %get-tuple-element.150, s32[4096,32]{0,1:T(8,128)S(1)} %constant_dynamic-slice_fusion.2, pred[]{:T(512)S(6)} %compare.3, bf16[4096,64,1]{0,1,2:T(8,128)(2,1)S(1)} %fusion.19), kind=kOutput, calls=%fused_computation.3.clone.3 | convolution fusion | flops 4329570304 | bytes 5242881 | tf_op jit(solution)/shard_map/while/body/eval_jaxpr/rk,rjb->jkb/dot_general | solution.py:70
  82.2 1.1 constant_dynamic-slice_fusion.2
  83.3 30.4 %bitcast_add_fusion.2 = f32[32,64,256]{2,1,0:T(8,128)} fusion(f32[32,64,256]{2,1,0:T(8,128)} %get-tuple-element.150, s32[4096,32]{0,1:T(8,128)S(1)} %constant_dynamic-slice_fusion.2, pred[]{:T(512)S(6)} %compare.3, bf16[4096,64,1]{0,1,2:T(8,128)(2,1)S(1)} %fusion.19), kind=kOutput, calls=%fused_computation.3.clone.3 | convolution fusion | flops 4329570304 | bytes 5242881 | tf_op jit(solution)/shard_map/while/body/eval_jaxpr/rk,rjb->jkb/dot_general | solution.py:70
  113.7 1.1 constant_dynamic-slice_fusion.2
  114.8 30.4 %bitcast_add_fusion.2 = f32[32,64,256]{2,1,0:T(8,128)} fusion(f32[32,64,256]{2,1,0:T(8,128)} %get-tuple-element.150, s32[4096,32]{0,1:T(8,128)S(1)} %constant_dynamic-slice_fusion.2, pred[]{:T(512)S(6)} %compare.3, bf16[4096,64,1]{0,1,2:T(8,128)(2,1)S(1)} %fusion.19), kind=kOutput, calls=%fused_computation.3.clone.3 | convolution fusion | flops 4329570304 | bytes 5242881 | tf_op jit(solution)/shard_map/while/body/eval_jaxpr/rk,rjb->jkb/dot_general | solution.py:70
  145.2 1.1 constant_dynamic-slice_fusion.2
  146.3 30.4 %bitcast_add_fusion.2 = f32[32,64,256]{2,1,0:T(8,128)} fusion(f32[32,64,256]{2,1,0:T(8,128)} %get-tuple-element.150, s32[4096,32]{0,1:T(8,128)S(1)} %constant_dynamic-slice_fusion.2, pred[]{:T(512)S(6)} %compare.3, bf16[4096,64,1]{0,1,2:T(8,128)(2,1)S(1)} %fusion.19), kind=kOutput, calls=%fused_computation.3.clone.3 | convolution fusion | flops 4329570304 | bytes 5242881 | tf_op jit(solution)/shard_map/while/body/eval_jaxpr/rk,rjb->jkb/dot_general | solution.py:70
  176.7 2.8 slice_bitcast_fusion.1
  179.5 0.5 reshape.125
  180.0 0.1 copy.69
  180.1 36.3 %reduce-window.14 = f32[32,2,16,2,128]{4,2,3,1,0:T(8,128)S(1)} reduce-window(f32[32,2,16,2,128]{4,2,3,1,0:T(8,128)S(1)} %copy.69, f32[]{:T(128)} %constant.40.clone.1), window={size=1x1x1x1x128 pad=0_0x0_0x0_0x0_0x127_0}, to_apply=%region_2.0 | reduce-window | flops 33292288 | bytes 2097156 | tf_op jit(solution)/shard_map/reduce-window
  216.4 0.3 slice.43
  216.7 0.6 copy.70
  217.4 0.1 fusion.9
  217.5 0.1 copy.71
  217.6 0.0 copy-done.1
  217.6 0.5 reshape.127
  218.2 0.1 copy.74
  218.3 36.3 %reduce-window.16 = f32[32,2,16,2,128]{4,2,3,1,0:T(8,128)S(1)} reduce-window(f32[32,2,16,2,128]{4,2,3,1,0:T(8,128)S(1)} %copy.74, f32[]{:T(128)} %constant.40.clone.1), window={size=1x1x1x1x128 pad=0_0x0_0x0_0x0_0x127_0}, to_apply=%region_4.5 | reduce-window | flops 33292288 | bytes 2097156 | tf_op jit(solution)/shard_map/reduce-window.2
  254.6 0.3 slice.46
  254.9 0.6 copy.75
  255.5 0.1 fusion.7
  255.7 0.1 copy.76
  255.8 1.8 broadcast_add_fusion
  257.6 3.2 %copy.88 = f32[32,2,16,2,128]{0,2,4,3,1:T(8,128)} copy(f32[32,2,16,2,128]{4,2,3,1,0:T(8,128)S(1)} %get-tuple-element.115) | data formatting | bytes 2097152 | tf_op jit(solution)/shard_map/reduce_window_sum
  260.8 0.6 copy.72
  261.4 3.3 %copy.89 = f32[32,2,16,2,128]{0,2,4,3,1:T(8,128)} copy(f32[32,2,16,2,128]{4,2,3,1,0:T(8,128)S(1)} %get-tuple-element.114) | data formatting | bytes 2097152 | tf_op jit(solution)/shard_map/reduce_window_sum
  264.7 0.7 slice_bitcast_fusion.3
  265.4 0.1 copy.80
  265.5 0.1 copy.83
  265.6 0.1 copy.84
  265.7 0.6 subtract_reduce_fusion
  266.3 1.5 copy.77
  267.8 40.2 %pmax.7 = f32[2,16]{1,0:T(2,128)} all-reduce(f32[2,16]{1,0:T(2,128)S(1)} %subtract_reduce_fusion), channel_id=1, replica_groups=mesh['rows'=8,'feat'=4] {'rows','feat'}, use_global_device_ids=true, to_apply=%region_7.8 | all-reduce | flops 32 | bytes 256 | tf_op jit(solution)/shard_map/pmax | solution.py:76
  308.0 0.8 reduce_window_sum.48
  308.8 2.1 reduce_window_sum.50
  310.9 1.4 add_subtract_fusion
  (19 shorter events, 0.2 us)
Async XLA Ops:
  3.6 5.3 %copy-start.2 = (s32[2,2048]{1,0:T(2,128)S(1)}, s32[2,2048]{1,0:T(2,128)}, u32[]{:S(2)}) copy-start(s32[2,2048]{1,0:T(2,128)} %param.8) | copy-start | bytes 49156
  3.6 5.4 %copy-start.3 = (s32[2,2048]{1,0:T(2,128)S(1)}, s32[2,2048]{1,0:T(2,128)}, u32[]{:S(2)}) copy-start(s32[2,2048]{1,0:T(2,128)} %param.7) | copy-start | bytes 49156
  3.6 35.7 %copy-start.4 = (bf16[2048]{0:T(1024)(128)(2,1)S(1)}, bf16[2048]{0:T(1024)(128)(2,1)}, u32[]{:S(2)}) copy-start(bf16[2048]{0:T(1024)(128)(2,1)} %param.9) | copy-start | bytes 12292
  3.6 44.6 %all-to-all-start = ((s32[2048,8,32]{0,2,1:T(8,128)}), s32[2048,8,32]{0,2,1:T(8,128)}, u32[]{:S(2)}, u32[]{:S(2)}) async-start(s32[2048,8,32]{0,2,1:T(8,128)} %bitcast), calls=%async_computation | async-start | bytes 4194304 | tf_op jit(solution)/shard_map/all_to_all | solution.py:49
  216.4 1.2 copy-start.1
  254.6 1.1 copy-start
where the time goes:
time: 313 us; the launch traced here: 312 us
  matrix products  121 us (39%)
  blocking collectives  78.6 us (25%)
  other arithmetic  78.2 us (25%)
  local copies, waits for them, and re-layouts  28.5 us (9%)
  starting transfers between devices  5.34 us (2%)
    dot_general x4, matrix products, add_block(): jnp.einsum('rk,rjb->jkb', cols, bin_hot, preferred_element_type=jnp.float32)  121 us
    another operation x5, other arithmetic  74.6 us
    pmax x1, blocking collectives, per_device(): best_gain = lax.pmax(local_best, ('rows', 'feat'))  40.2 us
    all_gather x1, blocking collectives, per_device(): lax.all_gather(jnp.concatenate([node_ids, boot_counts], axis=0), 'rows',...  30.2 us
    another operation x14, local copies, waits for them, and re-layouts  13.3 us
    all_gather x1, blocking collectives, per_device(): all_gradient = lax.all_gather(gradient, 'rows', axis=0, tiled=True)  8.22 us
  transfers between devices with their start and end apart: 1, of which 0 were waited for; matrix products, arithmetic and copies ran while one was open for 0% of the time, Pallas kernels for 0%

commit v1 on v0

v1 whole, which is shorter than its diff:
```python
import functools
import math

import jax
import jax.numpy as jnp
from jax import lax
from jax.experimental import pallas as pl
from jax.experimental.pallas import tpu as pltpu
from jax.sharding import PartitionSpec as P

BINS = 256
NODES = 16
RIDGE = 1.0
F8 = jnp.float8_e4m3fn
F32 = jnp.float32
BF16 = jnp.bfloat16
MESH = pl.DeviceIdType.MESH
NT = (((1,), (1,)), ((), ()))


def partner(me, step, count):
    if count & (count - 1):
        return lax.rem(me + step, count)
    out = me
    bit = 1
    while bit < count:
        if step & bit:
            out = out + bit * (1 - 2 * lax.rem(me // bit, 2))
        bit *= 2
    return out


def kernel(
    n, nf, trees, bins_ref, lab_ref, gains_ref, best_ref,
    got, labels, binsf, cols, acc, row_out, row_in,
    send_b, recv_b, send_l, recv_l, send_m, recv_m,
):
    _, owned, rows = bins_ref.shape
    wide = trees * NODES
    total = n * nf
    me, mf = lax.axis_index("rows"), lax.axis_index("feat")

    barrier = pltpu.get_barrier_semaphore()

    def greet(j, _):
        to = {"rows": lax.rem(me + j // nf, n), "feat": lax.rem(mf + j % nf, nf)}
        pl.semaphore_signal(barrier, inc=1, device_id=to, device_id_type=MESH)
        return 0

    lax.fori_loop(1, total, greet, 0)
    pl.semaphore_wait(barrier, total - 1)

    def label_copy(k, to):
        return pltpu.make_async_remote_copy(
            src_ref=lab_ref, dst_ref=labels.at[k], send_sem=send_l.at[k],
            recv_sem=recv_l.at[k], device_id={"rows": to}, device_id_type=MESH)

    def bins_copy(k, to):
        return pltpu.make_async_remote_copy(
            src_ref=bins_ref.at[to], dst_ref=got.at[k], send_sem=send_b.at[k],
            recv_sem=recv_b.at[k], device_id={"rows": to}, device_id_type=MESH)

    for k in range(1, n):
        to = partner(me, k, n)
        label_copy(k, to).start()
        bins_copy(k, to).start()

    got[0] = bins_ref[me]
    labels[0] = lab_ref[...]
    acc[...] = jnp.zeros_like(acc)

    chunk = math.gcd(512, rows)
    unroll = math.gcd(8, owned)
    edges = lax.broadcasted_iota(jnp.int32, (BINS, chunk), 0).astype(BF16)
    node_of = lax.broadcasted_iota(jnp.int32, (NODES, chunk), 0).astype(F32)
    one, zero = BF16(1), BF16(0)

    def block(k, _):
        @pl.when(k > 0)
        def _():
            to = lax.rem(me + 1, n)
            label_copy(k, to).wait_recv()
            bins_copy(k, to).wait_recv()

        binsf[...] = got[k].astype(F32)
        lab = labels[k].astype(F32)
        counts = lab[trees:2 * trees]
        weighted = (counts * lab[2 * trees:2 * trees + 1]).astype(BF16).astype(F32)
        for c in range(0, rows, chunk):
            span = slice(c, c + chunk)
            hot = [lab[t:t + 1, span] == node_of for t in range(trees)]

            def spread(values):
                return jnp.concatenate(
                    [jnp.where(hot[t], values[t:t + 1, span], 0.0) for t in range(trees)], axis=0)

            cols[0:wide, span] = spread(weighted).astype(BF16)
            cols[wide:2 * wide, span] = spread(counts).astype(BF16)

        def features(g, _):
            for u in range(unroll):
                f = g * unroll + u
                hist = None
                for c in range(0, rows, chunk):
                    row = binsf[pl.ds(f, 1), c:c + chunk].astype(BF16)
                    mask = jnp.where(row <= edges, one, zero).astype(F8)
                    part = lax.dot_general(
                        cols[:, c:c + chunk], mask, NT, preferred_element_type=F32)
                    hist = part if hist is None else hist + part
                acc[f] += hist
            return 0

        lax.fori_loop(0, owned // unroll, features, 0)
        return 0

    lax.fori_loop(0, n, block, 0)

    def finish(f, top):
        left_grad = acc[f, 0:wide]
        left_count = acc[f, wide:2 * wide]
        total_grad = left_grad[:, BINS - 1:BINS]
        total_count = left_count[:, BINS - 1:BINS]
        right_grad = total_grad - left_grad
        right_count = total_count - left_count
        gain = (
            left_grad * left_grad / (left_count + RIDGE)
            + right_grad * right_grad / (right_count + RIDGE)
            - total_grad * total_grad / (total_count + RIDGE)
        )
        gains_ref[f] = gain
        return jnp.maximum(top, gain)

    top = lax.fori_loop(0, owned, finish, jnp.full((wide, BINS), -jnp.inf, F32))
    top = jnp.max(top, axis=1, keepdims=True)
    diagonal = (
        lax.broadcasted_iota(jnp.int32, (wide, 128), 0)
        == lax.broadcasted_iota(jnp.int32, (wide, 128), 1)
    )
    row = jnp.max(jnp.where(diagonal, top, -jnp.inf), axis=0, keepdims=True)
    row_out[...] = row
    row_in[0] = row

    def row_copy(j):
        to = {"rows": lax.rem(me + j // nf, n), "feat": lax.rem(mf + j % nf, nf)}
        return pltpu.make_async_remote_copy(
            src_ref=row_out, dst_ref=row_in.at[j], send_sem=send_m.at[j],
            recv_sem=recv_m.at[j], device_id=to, device_id_type=MESH)

    def send_row(j, _):
        row_copy(j).start()
        return 0

    lax.fori_loop(1, total, send_row, 0)

    for k in range(1, n):
        to = partner(me, k, n)
        label_copy(k, to).wait_send()
        bins_copy(k, to).wait_send()

    def take_row(j, _):
        row_copy(j).wait_send()
        row_copy(j).wait_recv()
        return 0

    lax.fori_loop(1, total, take_row, 0)
    best_ref[...] = jnp.max(row_in[...], axis=0)


def per_device(n, nf, bins, node_ids, boot_counts, gradient):
    rows, feat_local = bins.shape
    trees = node_ids.shape[0]
    owned = feat_local // n
    wide = trees * NODES
    by_owner = bins.astype(BF16).T.reshape(n, owned, rows)
    labels = jnp.concatenate(
        [node_ids.astype(BF16), boot_counts.astype(BF16), gradient[None]], axis=0)
    tall = -(-labels.shape[0] // 8) * 8
    labels = jnp.pad(labels, ((0, tall - labels.shape[0]), (0, 0)))
    total = n * nf
    vmem = pl.BlockSpec(memory_space=pltpu.VMEM)
    gains, best = pl.pallas_call(
        functools.partial(kernel, n, nf, trees),
        out_shape=(
            jax.ShapeDtypeStruct((owned, wide, BINS), F32),
            jax.ShapeDtypeStruct((1, 128), F32),
        ),
        in_specs=[vmem, vmem],
        out_specs=(vmem, vmem),
        scratch_shapes=[
            pltpu.VMEM((n, owned, rows), BF16),
            pltpu.VMEM((n, tall, rows), BF16),
            pltpu.VMEM((owned, rows), F32),
            pltpu.VMEM((2 * wide, rows), BF16),
            pltpu.VMEM((owned, 2 * wide, BINS), F32),
            pltpu.VMEM((1, 128), F32),
            pltpu.VMEM((total, 1, 128), F32),
            pltpu.SemaphoreType.DMA((n,)),
            pltpu.SemaphoreType.DMA((n,)),
            pltpu.SemaphoreType.DMA((n,)),
            pltpu.SemaphoreType.DMA((n,)),
            pltpu.SemaphoreType.DMA((total,)),
            pltpu.SemaphoreType.DMA((total,)),
        ],
        compiler_params=pltpu.CompilerParams(
            collective_id=0, has_side_effects=True, vmem_limit_bytes=48 * 2**20),
    )(by_owner, labels)
    gains = gains.reshape(1, owned, trees, NODES, BINS)
    return gains, best[0, :wide].reshape(trees, NODES)


def solution(mesh):
    n, nf = mesh.shape["rows"], mesh.shape["feat"]
    in_specs = (P("rows", "feat"), P(None, "rows"), P(None, "rows"), P("rows"))
    out_specs = (P("feat", "rows", None, None, None), P())
    return jax.shard_map(
        functools.partial(per_device, n, nf),
        mesh=mesh, in_specs=in_specs, out_specs=out_specs, check_vma=False)
```

time: 313 us -> 72.3 us (0.23)
  matrix products: 121 us -> 0 us
  blocking collectives: 78.6 us -> 0 us
  other arithmetic: 78.2 us -> 3.25 us
  Pallas kernels: 0 us -> 65 us
  local copies, waits for them, and re-layouts: 28.5 us -> 2.97 us
  starting transfers between devices: 5.34 us -> 0 us
    dot_general x4 -> x0, matrix products: 121 us -> none  [add_block(): jnp.einsum('rk,rjb->jkb', cols, bin_hot, preferred_element_type=jnp.float32)]
    another operation x6 -> x0, other arithmetic: 74.8 us -> none
    pallas_call x0 -> x1, Pallas kernels: none -> 65 us  [per_device(): pl.pallas_call(functools.partial(kernel, n, nf, trees), out_shape=(jax.Sh...]
    pmax x1 -> x0, blocking collectives: 40.2 us -> none  [per_device(): best_gain = lax.pmax(local_best, ('rows', 'feat'))]
    all_gather x2 -> x0, blocking collectives: 38.4 us -> none  [the longest x1 30.2 us: per_device(): lax.all_gather(jnp.concatenate([node_ids, boot_counts], axis=0), 'rows',...]
    another operation x14 -> x1, local copies, waits for them, and re-layouts: 13.3 us -> 0.65 us  [per_device(): return (gains, best[0, :wide].reshape(trees, NODES))]
    all_to_all x1 -> x0, starting transfers between devices: 5.34 us -> none  [per_device(): lax.all_to_all(bins, 'rows', split_axis=1, concat_axis=0, tiled=True)]
    unnamed x12 -> x1, local copies, waits for them, and re-layouts: 5.74 us -> 0.97 us
  transfers between devices with their start and end apart: 1 -> 0, of which waited for: 0 -> 0; matrix products, arithmetic and copies ran while one was open for 0% -> 0% of each run, Pallas kernels for 0% -> 0%
where the time goes in v1:
time: 72.3 us; the launch traced here: 71.9 us
  Pallas kernels  65 us (90%)
  other arithmetic  3.25 us (4%)
  local copies, waits for them, and re-layouts  2.97 us (4%)
    pallas_call x1, Pallas kernels, per_device(): pl.pallas_call(functools.partial(kernel, n, nf, trees), out_shape=(jax.Sh...  65 us
    transpose x1, other arithmetic, per_device(): by_owner = bins.astype(BF16).T.reshape(n, owned, rows)  1.76 us

profile of v1, /device:TPU:0, one launch (start us, length us, event | category | flops | bytes accessed | tf_op | source)
XLA Modules:
  0.0 71.9 jit_solution(13472291892870042873)
XLA Ops:
  0.6 0.7 %convert_element_type.12 = bf16[2,2048]{1,0:T(2,128)(2,1)S(1)} convert(s32[2,2048]{1,0:T(2,128)} %param.5) | non-fusion elementwise | flops 4096 | bytes 24576 | tf_op jit(solution)/shard_map/convert_element_type | solution.py:176
  1.4 0.7 %convert_element_type.13 = bf16[2,2048]{1,0:T(2,128)(2,1)S(1)} convert(s32[2,2048]{1,0:T(2,128)} %param.6) | non-fusion elementwise | flops 4096 | bytes 24576 | tf_op jit(solution)/shard_map/convert_element_type | solution.py:176
  2.1 0.7 broadcast_in_dim.3
  2.8 1.8 %convert_bitcast_fusion = bf16[256,2048]{0,1:T(8,128)(2,1)S(1)} fusion(s32[2048,256]{1,0:T(8,128)} %param.4), kind=kLoop, calls=%fused_computation | loop fusion | flops 524288 | bytes 3145728 | tf_op jit(solution)/shard_map/transpose | solution.py:174
  4.6 0.6 copy.6
  5.2 65.0 %shard_map.59 = (f32[32,32,256]{2,1,0:T(8,128)S(1)}, f32[1,128]{1,0:T(1,128)S(1)}) custom-call(bf16[8,32,2048]{2,1,0:T(8,128)(2,1)S(1)} %bitcast.4, bf16[8,2048]{1,0:T(8,128)(2,1)S(1)} %fusion.4.lab_ref), custom_call_target="tpu_custom_call" | custom-call | tf_op jit(solution)/shard_map/pallas_call | solution.py:181
  70.3 0.6 reshape_squeeze.3
  70.9 1.0 %copy.8 = f32[1,32,2,16,256]{4,3,2,1,0:T(8,128)} copy(f32[1,32,2,16,256]{4,3,2,1,0:T(8,128)S(1)} %bitcast.5) | data formatting | bytes 2097152
  (2 shorter events, 0.1 us)
